TPU v7x, 8 devices: a whole 2x2x1 slice. The times are simulated.
8 devices in a mesh: rhs: 1 (over z), col: 2 (over y), row: 4 (over x, core).
Axes of the slice: x: 2, y: 2, z: 1, core: 2. Of those that a mesh axis runs over, the one named last changes fastest.
Arguments:
- volume: bfloat16 [128, 128, 128, 64], P('row', 'col', None, 'rhs')
- a_one: bfloat16 [128, 128], replicated
- b_one: bfloat16 [128, 128], replicated
- a_two: bfloat16 [128, 128], replicated
- b_two: bfloat16 [128, 128], replicated
- a_three: bfloat16 [128, 128], replicated
- b_three: bfloat16 [128, 128], replicated
- spectrum: float32 [128, 128, 128], P('row', 'col')
Outputs:
- output: float32 [128, 128, 128, 64], P('row', 'col', None, 'rhs')
All inputs are finite; a program needn't handle non-finite values.
Results may differ from a plain program's by a relative error of at most 0.0126449.
Values are sent between devices in bfloat16 or wider.
A program may use at most 1 GiB of HBM per device.

v0:
```python
import jax
import jax.numpy as jnp
from jax import lax
from jax.sharding import PartitionSpec as P


def mode_product(factor, tensor, form):
    return jnp.einsum(form, factor, tensor, preferred_element_type=jnp.float32)


def solution(mesh):
    vol_spec = P('row', 'col', None, 'rhs')
    diag_spec = P('row', 'col', None)
    full_spec = P(None, None)

    def local_op(volume, a_one, b_one, a_two, b_two, a_three, b_three, spectrum):
        u_three = mode_product(a_three, volume, 'ka,ijar->ijkr').astype(jnp.bfloat16)
        one_whole = lax.all_to_all(u_three, 'row', 2, 0, tiled=True)
        u_one = mode_product(a_one, one_whole, 'ia,ajkr->ijkr').astype(jnp.bfloat16)
        two_whole = lax.all_to_all(u_one, 'col', 0, 1, tiled=True)
        u_two = mode_product(a_two, two_whole, 'ja,iakr->ijkr').astype(jnp.bfloat16)
        diag_mid = lax.all_to_all(spectrum, 'row', 2, 0, tiled=True)
        diag_new = lax.all_to_all(diag_mid, 'col', 0, 1, tiled=True)
        scaled = (diag_new[:, :, :, None] * u_two.astype(jnp.float32)).astype(jnp.bfloat16)
        v_two = mode_product(b_two, scaled, 'ja,iakr->ijkr').astype(jnp.bfloat16)
        one_again = lax.all_to_all(v_two, 'col', 1, 0, tiled=True)
        v_one = mode_product(b_one, one_again, 'ia,ajkr->ijkr').astype(jnp.bfloat16)
        three_whole = lax.all_to_all(v_one, 'row', 0, 2, tiled=True)
        return mode_product(b_three, three_whole, 'ka,ijar->ijkr')

    return jax.shard_map(local_op, mesh=mesh, in_specs=(vol_spec, full_spec, full_spec, full_spec, full_spec, full_spec, full_spec, diag_spec), out_specs=vol_spec, check_vma=False)
```

profile of v0, /device:TPU:0, one launch (start us, length us, event | category | flops | bytes accessed | tf_op | source)
XLA Modules:
  0.0 3313.7 jit_solution(5700673788281223678)
XLA Ops:
  0.0 0.0 copy-start
  0.0 3.1 copy.35
  3.1 2.4 reshape.8
  5.5 4.6 all-to-all-start
  10.1 0.0 copy-done
  10.1 23.3 convert_bitcast_fusion.3
  33.4 89.9 %copy.40 = bf16[32,64,128,64]{3,1,0,2:T(8,128)(2,1)} copy(bf16[32,64,128,64]{2,3,1,0:T(8,128)(2,1)} %convert_bitcast_fusion.3) | data formatting | bytes 67108864 | tf_op jit(solution)/shard_map/convert_element_type | solution.py:17
  123.2 46.1 %reshape.12 = bf16[4,2,2097152]{2,1,0:T(2,128)(2,1)} reshape(bf16[128,32,64,64]{3,2,1,0:T(8,128)(2,1)} %bitcast.78) | data formatting | bytes 67108864
  169.3 0.0 all-to-all-done
  169.3 20.6 all-to-all-start.2
  189.9 0.6 broadcast
  190.5 3.7 reduce
  194.1 1.0 reshape.9
  195.1 2.5 copy.37
  197.7 3.3 reshape.10
  201.0 351.4 %all-to-all-done.2 = bf16[4,2,2097152]{2,1,0:T(2,128)(2,1)} async-done(((bf16[4,2,2097152]{2,1,0:T(2,128)(2,1)}), bf16[4,2,2097152]{2,1,0:T(2,128)(2,1)}, u32[]{:S(2)}, u32[]{:S(2)}) %all-to-all-start.2) | async-done | bytes 33554464 | tf_op jit(solution)/shard_map/all_to_all | solution.py:18
  552.4 4.4 all-to-all-start.1
  556.8 87.7 %reshape.13 = bf16[128,32,64,64]{3,2,1,0:T(8,128)(2,1)} reshape(bf16[4,2,2097152]{2,1,0:T(2,128)(2,1)} %all-to-all-done.2) | data formatting | bytes 67108864
  644.5 0.0 copy-start.4
  644.5 66.6 %copy.42 = bf16[4,32,64,32,64]{4,3,2,1,0:T(8,128)(2,1)} copy(bf16[4,32,64,32,64]{4,2,1,3,0:T(8,128)(2,1)} %bitcast.12) | data formatting | bytes 67108864 | tf_op jit(solution)/shard_map/all_to_all | solution.py:18
  711.1 0.0 copy-done.4
  711.1 45.0 %convert_bitcast_fusion.2 = bf16[128,64,32,64]{0,3,2,1:T(8,128)(2,1)} fusion(bf16[128,64,32,64]{3,2,1,0:T(8,128)(2,1)} %bitcast.13, bf16[128,128]{1,0:T(8,128)(2,1)S(1)} %copy-done.4), kind=kOutput, calls=%fused_computation.8 | convolution fusion | flops 4311744512 | bytes 67141632 | tf_op jit(solution)/shard_map/ia,ajkr->ijkr/dot_general | solution.py:8
  756.1 89.0 %copy.44 = bf16[128,64,32,64]{3,2,1,0:T(8,128)(2,1)} copy(bf16[128,64,32,64]{0,3,2,1:T(8,128)(2,1)} %convert_bitcast_fusion.2) | data formatting | bytes 67108864 | tf_op jit(solution)/shard_map/convert_element_type | solution.py:19
  845.1 55.7 %reshape.14 = bf16[2,2,4194304]{2,1,0:T(2,128)(2,1)} reshape(bf16[128,64,32,64]{3,2,1,0:T(8,128)(2,1)} %copy.44) | data formatting | bytes 67108864
  900.8 0.0 all-to-all-done.1
  900.8 13.1 all-to-all-start.3
  913.9 4.9 reduce.1
  918.8 1.2 reshape.11
  920.0 3.2 copy.67
  923.2 2.8 mul.10
  926.0 350.2 %all-to-all-done.3 = bf16[2,2,4194304]{2,1,0:T(2,128)(2,1)} async-done(((bf16[2,2,4194304]{2,1,0:T(2,128)(2,1)}), bf16[2,2,4194304]{2,1,0:T(2,128)(2,1)}, u32[]{:S(2)}, u32[]{:S(2)}) %all-to-all-start.3) | async-done | bytes 33554464 | tf_op jit(solution)/shard_map/all_to_all | solution.py:20
  1276.2 87.7 %reshape.15 = bf16[128,64,32,64]{3,2,1,0:T(8,128)(2,1)} reshape(bf16[2,2,4194304]{2,1,0:T(2,128)(2,1)} %all-to-all-done.3) | data formatting | bytes 67108864
  1363.9 178.7 %copy.45 = bf16[2,64,64,32,64]{2,0,4,3,1:T(2,128)(2,1)} copy(bf16[2,64,64,32,64]{4,3,2,1,0:T(8,128)(2,1)} %bitcast.17) | data formatting | bytes 67108864 | tf_op jit(solution)/shard_map/all_to_all | solution.py:20
  1542.6 0.0 copy-start.2
  1542.6 0.0 copy-start.5
  1542.6 103.5 %all_to_all.90 = bf16[64,128,32,64]{1,3,2,0:T(8,128)(2,1)} reshape(bf16[64,2,64,32,64]{2,1,4,3,0:T(2,128)(2,1)} %bitcast.18) | data formatting | bytes 67108864 | tf_op jit(solution)/shard_map/all_to_all | solution.py:20
  1646.1 0.0 copy-done.2
  1646.1 0.0 copy-done.5
  1646.1 40.3 %convert_bitcast_fusion.1 = bf16[64,128,32,64]{1,3,2,0:T(8,128)(2,1)} fusion(f32[64,128,32]{1,2,0:T(8,128)S(1)} %mul.10, bf16[64,128,32,64]{1,3,2,0:T(8,128)(2,1)} %all_to_all.90, bf16[128,128]{1,0:T(8,128)(2,1)S(1)} %copy-done.5, bf16[128,128]{1,0:T(8,128)(2,1)S(1)} %copy-done.2), kind=kOutput, calls=%fused_computation.6 | convolution fusion | flops 8673820672 | bytes 68222976 | tf_op jit(solution)/shard_map/ja,iakr->ijkr/dot_general | solution.py:8
  1686.3 89.0 %copy.46 = bf16[64,128,32,64]{3,2,0,1:T(8,128)(2,1)} copy(bf16[64,128,32,64]{1,3,2,0:T(8,128)(2,1)} %convert_bitcast_fusion.1) | data formatting | bytes 67108864 | tf_op jit(solution)/shard_map/convert_element_type | solution.py:25
  1775.3 55.3 %reshape.16 = bf16[2,2,4194304]{2,1,0:T(2,128)(2,1)} reshape(bf16[128,64,32,64]{3,2,1,0:T(8,128)(2,1)} %bitcast.80) | data formatting | bytes 67108864
  1830.6 394.0 %all_to_all.105 = bf16[2,2,4194304]{2,1,0:T(2,128)(2,1)} all-to-all(bf16[2,2,4194304]{2,1,0:T(2,128)(2,1)} %reshape.16), channel_id=1, replica_groups=mesh['rhs'=1,'col'=2,'row'=4] {'col'}, dimensions={0} | all-to-all | bytes 67108864 | tf_op jit(solution)/shard_map/all_to_all | solution.py:26
  2224.6 87.5 %reshape.17 = bf16[128,64,32,64]{3,2,1,0:T(8,128)(2,1)} reshape(bf16[2,2,4194304]{2,1,0:T(2,128)(2,1)} %all_to_all.105) | data formatting | bytes 67108864
  2312.1 178.7 %copy.47 = bf16[64,2,64,32,64]{0,1,4,3,2:T(2,128)(2,1)} copy(bf16[64,2,64,32,64]{4,3,0,2,1:T(8,128)(2,1)} %bitcast.25) | data formatting | bytes 67108864 | tf_op jit(solution)/shard_map/all_to_all | solution.py:26
  2490.8 0.0 copy-start.3
  2490.8 103.5 %all_to_all.94 = bf16[128,64,32,64]{0,3,2,1:T(8,128)(2,1)} reshape(bf16[2,64,64,32,64]{1,0,4,3,2:T(2,128)(2,1)} %bitcast.26) | data formatting | bytes 67108864 | tf_op jit(solution)/shard_map/all_to_all | solution.py:26
  2594.3 0.0 copy-done.3
  2594.3 23.2 convert_bitcast_fusion
  2617.5 89.0 %copy.48 = bf16[128,64,32,64]{3,2,1,0:T(8,128)(2,1)} copy(bf16[128,64,32,64]{0,3,2,1:T(8,128)(2,1)} %convert_bitcast_fusion) | data formatting | bytes 67108864 | tf_op jit(solution)/shard_map/convert_element_type | solution.py:27
  2706.5 46.1 %reshape.18 = bf16[4,2,2097152]{2,1,0:T(2,128)(2,1)} reshape(bf16[128,64,32,64]{3,2,1,0:T(8,128)(2,1)} %copy.48) | data formatting | bytes 67108864
  2752.6 380.8 %all_to_all.106 = bf16[4,2,2097152]{2,1,0:T(2,128)(2,1)} all-to-all(bf16[4,2,2097152]{2,1,0:T(2,128)(2,1)} %reshape.18), channel_id=1, replica_groups=mesh['rhs'=1,'col'=2,'row'=4] {'row'}, dimensions={0} | all-to-all | bytes 67108864 | tf_op jit(solution)/shard_map/all_to_all | solution.py:28
  3133.4 87.7 %reshape.19 = bf16[128,64,32,64]{3,2,1,0:T(8,128)(2,1)} reshape(bf16[4,2,2097152]{2,1,0:T(2,128)(2,1)} %all_to_all.106) | data formatting | bytes 67108864
  3221.1 0.0 copy-start.6
  3221.1 43.9 %copy.49 = bf16[32,64,4,32,64]{4,3,2,1,0:T(8,128)(2,1)} copy(bf16[32,64,4,32,64]{4,3,1,0,2:T(8,128)(2,1)} %bitcast.31) | data formatting | bytes 67108864 | tf_op jit(solution)/shard_map/all_to_all | solution.py:28
  3264.9 0.0 copy-done.6
  3264.9 0.0 copy-start.1
  3265.0 48.4 %convolution_bitcast_fusion = f32[32,64,128,64]{2,3,1,0:T(8,128)} fusion(bf16[32,64,128,64]{3,2,1,0:T(8,128)(2,1)} %bitcast.32, bf16[128,128]{1,0:T(8,128)(2,1)S(1)} %copy-done.6), kind=kOutput, calls=%fused_computation.11 | convolution fusion | flops 4294967296 | bytes 100696064 | tf_op jit(solution)/shard_map/ka,ijar->ijkr/dot_general | solution.py:8
  3313.3 0.0 copy-done.1
Async XLA Ops:
  0.0 10.1 copy-start
  5.5 163.8 %all-to-all-start = ((f32[4,1,65536]{2,1,0:T(1,128)}), f32[4,1,65536]{2,1,0:T(1,128)S(1)}, u32[]{:S(2)}, u32[]{:S(2)}) async-start(f32[4,1,65536]{2,1,0:T(1,128)} %reshape.8), calls=%async_computation | async-start | bytes 2097152 | tf_op jit(solution)/shard_map/all_to_all | solution.py:22
  169.3 383.1 %all-to-all-start.2 = ((bf16[4,2,2097152]{2,1,0:T(2,128)(2,1)}), bf16[4,2,2097152]{2,1,0:T(2,128)(2,1)}, u32[]{:S(2)}, u32[]{:S(2)}) async-start(bf16[4,2,2097152]{2,1,0:T(2,128)(2,1)} %reshape.12), calls=%async_computation.2 | async-start | bytes 67108864 | tf_op jit(solution)/shard_map/all_to_all | solution.py:18
  552.4 348.4 %all-to-all-start.1 = ((f32[2,1,131072]{2,1,0:T(1,128)}), f32[2,1,131072]{2,1,0:T(1,128)}, u32[]{:S(2)}, u32[]{:S(2)}) async-start(f32[2,1,131072]{2,1,0:T(1,128)} %reshape.10), calls=%async_computation.1 | async-start | bytes 2097152 | tf_op jit(solution)/shard_map/all_to_all | solution.py:23
  644.5 66.6 %copy-start.4 = (bf16[128,128]{1,0:T(8,128)(2,1)S(1)}, bf16[128,128]{1,0:T(8,128)(2,1)}, u32[]{:S(2)}) copy-start(bf16[128,128]{1,0:T(8,128)(2,1)} %param.9) | copy-start | bytes 98308
  900.8 375.4 %all-to-all-start.3 = ((bf16[2,2,4194304]{2,1,0:T(2,128)(2,1)}), bf16[2,2,4194304]{2,1,0:T(2,128)(2,1)}, u32[]{:S(2)}, u32[]{:S(2)}) async-start(bf16[2,2,4194304]{2,1,0:T(2,128)(2,1)} %reshape.14), calls=%async_computation.3 | async-start | bytes 67108864 | tf_op jit(solution)/shard_map/all_to_all | solution.py:20
  1542.6 103.5 %copy-start.2 = (bf16[128,128]{1,0:T(8,128)(2,1)S(1)}, bf16[128,128]{1,0:T(8,128)(2,1)}, u32[]{:S(2)}) copy-start(bf16[128,128]{1,0:T(8,128)(2,1)} %param.11) | copy-start | bytes 98308
  1542.6 103.5 %copy-start.5 = (bf16[128,128]{1,0:T(8,128)(2,1)S(1)}, bf16[128,128]{1,0:T(8,128)(2,1)}, u32[]{:S(2)}) copy-start(bf16[128,128]{1,0:T(8,128)(2,1)} %param.12) | copy-start | bytes 98308
  2490.8 103.5 %copy-start.3 = (bf16[128,128]{1,0:T(8,128)(2,1)S(1)}, bf16[128,128]{1,0:T(8,128)(2,1)}, u32[]{:S(2)}) copy-start(bf16[128,128]{1,0:T(8,128)(2,1)} %param.10) | copy-start | bytes 98308
  3221.1 43.9 %copy-start.6 = (bf16[128,128]{1,0:T(8,128)(2,1)S(1)}, bf16[128,128]{1,0:T(8,128)(2,1)}, u32[]{:S(2)}) copy-start(bf16[128,128]{1,0:T(8,128)(2,1)} %param.14) | copy-start | bytes 98308
  3264.9 48.4 %copy-start.1 = (bf16[128,128]{1,0:T(8,128)(2,1)S(1)}, bf16[128,128]{1,0:T(8,128)(2,1)}, u32[]{:S(2)}) copy-start(bf16[128,128]{1,0:T(8,128)(2,1)} %param.13) | copy-start | bytes 98308
where the time goes:
time: 3340 us; the launch traced here: 3310 us
  local copies, waits for them, and re-layouts  1610 us (48%)
  blocking collectives  775 us (23%)
  waiting for transfers between devices  702 us (21%)
  matrix products  180 us (5%)
  starting transfers between devices  42.8 us (1%)
    unnamed x27, local copies, waits for them, and re-layouts  565 us
    all_to_all x1, blocking collectives, local_op(): one_again = lax.all_to_all(v_two, 'col', 1, 0, tiled=True)  394 us
    all_to_all x1, blocking collectives, local_op(): three_whole = lax.all_to_all(v_one, 'row', 0, 2, tiled=True)  381 us
    all_to_all x1, waiting for transfers between devices, local_op(): one_whole = lax.all_to_all(u_three, 'row', 2, 0, tiled=True)  351 us
    all_to_all x1, waiting for transfers between devices, local_op(): two_whole = lax.all_to_all(u_one, 'col', 0, 1, tiled=True)  350 us
    all_to_all x2, local copies, waits for them, and re-layouts, local_op(): two_whole = lax.all_to_all(u_one, 'col', 0, 1, tiled=True)  282 us
    all_to_all x2, local copies, waits for them, and re-layouts, local_op(): one_again = lax.all_to_all(v_two, 'col', 1, 0, tiled=True)  282 us
    dot_general x5, matrix products, mode_product(): return jnp.einsum(form, factor, tensor, preferred_element_type=jnp.float32)  180 us
  transfers between devices with their start and end apart: 4, of which 2 were waited for; matrix products, arithmetic and copies ran while one was open for 16% of the time, Pallas kernels for 0%

commit v1 on v0

v1 whole, which is shorter than its diff:
```python
import functools

import jax
import jax.numpy as jnp
from jax import lax
from jax.experimental import pallas as pl
from jax.experimental.pallas import tpu as pltpu
from jax.sharding import PartitionSpec as P

F32 = jnp.float32
BF16 = jnp.bfloat16
MESH = pl.DeviceIdType.MESH
ND = 8
JB = 4
PA = 72
PB = 136
JC = 2


def dot(a, b):
    return jnp.dot(a, b, preferred_element_type=F32)


def exchange_kernel(x, w3, a1, a2, b2, b1, d, u3, recv, vs, q,
                    xb, ub, ta, p, u1, v2, vo, tb, dv,
                    xsem, usem, psem, vsem, dsem, dss, drs, oss, ors, rss, rrs):
    row, col = lax.axis_index('row'), lax.axis_index('col')
    me = col * 4 + row

    def peer(s):
        return {'row': row ^ (s & 3), 'col': col ^ (s >> 2)}

    def idx(s):
        return (col ^ (s >> 2)) * 4 + (row ^ (s & 3))

    def rows_of(s):
        return pl.ds(pl.multiple_of((row ^ (s & 3)) * 32, 32), 32)

    def cols_of(s):
        return pl.ds(pl.multiple_of((col ^ (s >> 2)) * 64, 64), 64)

    def remote(src, dst, send, recv_, s):
        return pltpu.make_async_remote_copy(
            src_ref=src, dst_ref=dst, send_sem=send, recv_sem=recv_,
            device_id=peer(s), device_id_type=MESH)

    bar = pltpu.get_barrier_semaphore()
    for s in range(1, ND):
        pl.semaphore_signal(bar, inc=1, device_id=peer(s), device_id_type=MESH)
    pl.semaphore_wait(bar, ND - 1)

    own_d = pltpu.make_async_copy(d, dv.at[rows_of(0), cols_of(0), :], dsem)
    own_d.start()

    def d_out(s):
        return remote(d, dv.at[rows_of(0), cols_of(0), :], dss.at[s], drs.at[s], s)

    def d_in(s):
        return remote(d, dv.at[rows_of(s), cols_of(s), :], dss.at[s], drs.at[s], s)

    for s in (2, 4, 6):
        d_out(s).start()

    def x_load(c, t, slot):
        return pltpu.make_async_copy(
            x.at[:, pl.ds(t * JB, JB), pl.ds(pl.multiple_of(c * 16, 16), 16), :],
            xb.at[slot], xsem.at[slot])

    def u_store(c, t, slot):
        return pltpu.make_async_copy(
            ub.at[slot], u3.at[c, :, pl.ds(t * JB, JB), :, :], usem.at[slot])

    def out_copy(ch, s):
        return remote(u3.at[ch // 2, (ch % 2) * 8 + idx(s)], recv.at[ch, me],
                      oss.at[ch, s], ors.at[ch, s], s)

    def out_arrival(ch, s):
        return remote(u3.at[ch // 2, (ch % 2) * 8 + idx(s)], recv.at[ch, idx(s)],
                      oss.at[ch, s], ors.at[ch, s], s)

    nt = 64 // JB

    def group(c, carry):
        x_load(c, 0, 0).start()

        def block(t, carry):
            slot = lax.rem(t, 2)

            @pl.when(t + 1 < nt)
            def _():
                x_load(c, t + 1, 1 - slot).start()

            x_load(c, t, slot).wait()

            @pl.when(t >= 2)
            def _():
                u_store(c, t - 2, slot).wait()

            lo = xb[slot, 0:16].reshape(16 * JB * 16, 128)
            hi = xb[slot, 16:32].reshape(16 * JB * 16, 128)
            y = dot(jnp.concatenate([lo, hi], axis=1), w3[...])
            n = JB * 16
            for i in range(16):
                ta[i * PA:i * PA + n, :] = y[i * n:(i + 1) * n, :128]
                ta[(i + 16) * PA:(i + 16) * PA + n, :] = y[i * n:(i + 1) * n, 128:]

            for r in range(16):
                for j in range(JB):
                    ub[slot, r, j] = ta[pl.ds(j * 16 + r, 32, stride=PA), :].astype(BF16)
            u_store(c, t, slot).start()
            return carry

        lax.fori_loop(0, nt, block, 0)
        u_store(c, nt - 2, (nt - 2) % 2).wait()
        u_store(c, nt - 1, (nt - 1) % 2).wait()
        for h in range(2):
            for s in range(1, ND):
                out_copy(2 * c + h, s).start()
        return carry

    lax.fori_loop(0, 4, group, 0)

    own_d.wait()
    for s in (2, 4, 6):
        d_in(s).wait_recv()

    def d_relay(s):
        return remote(dv.at[rows_of(s), cols_of(s), :], dv.at[rows_of(s), cols_of(s), :],
                      dss.at[s + 1], drs.at[s + 1], 1)

    def d_relayed(s):
        return remote(dv.at[rows_of(s), cols_of(s), :], dv.at[rows_of(s + 1), cols_of(s + 1), :],
                      dss.at[s + 1], drs.at[s + 1], 1)

    for s in (0, 2, 4, 6):
        d_relay(s).start()
    for s in (0, 2, 4, 6):
        d_relayed(s).wait_recv()

    def back_copy(ch, s):
        return remote(vs.at[ch, s], q.at[ch, me], rss.at[ch, s], rrs.at[ch, s], s)

    def back_arrival(ch, s):
        return remote(vs.at[ch, s], q.at[ch, idx(s)], rss.at[ch, s], rrs.at[ch, s], s)

    def swap_out(dst, g):
        def body(i, carry):
            for e in range(16):
                n = i * 16 + e
                dst[n, pl.ds(pl.multiple_of(g * 16, 16), 16), :] = (
                    tb[pl.ds(n, 16, stride=PB), :].astype(BF16))
            return carry
        lax.fori_loop(0, 8, body, 0)

    def chunk(ch, carry):
        for s in range(1, ND):
            out_arrival(ch, s).wait_recv()
        loads = []
        for s in range(ND):
            src = recv.at[ch, idx(s)] if s else u3.at[ch // 2, (ch % 2) * 8 + me]
            loads.append(pltpu.make_async_copy(
                src, p.at[cols_of(s), rows_of(s), :], psem.at[s]))
            loads[-1].start()
        for load in loads:
            load.wait()

        def one(g, carry):
            for e in range(8):
                j = g * 16 + 2 * e
                y = dot(a1[...], jnp.concatenate([p[j], p[j + 1]], axis=1))
                tb[2 * e * PB:2 * e * PB + 128, :] = y[:, :128]
                tb[(2 * e + 1) * PB:(2 * e + 1) * PB + 128, :] = y[:, 128:]
            swap_out(u1, g)
            return carry

        lax.fori_loop(0, 8, one, 0)

        def two(g, carry):
            for e in range(8):
                i = g * 16 + 2 * e
                y = dot(a2[...], jnp.concatenate([u1[i], u1[i + 1]], axis=1))
                y = y.astype(BF16).astype(F32)
                w = jnp.concatenate([dv[i], dv[i + 1]], axis=1) * y
                z = dot(b2[...], w.astype(BF16))
                tb[2 * e * PB:2 * e * PB + 128, :] = z[:, :128]
                tb[(2 * e + 1) * PB:(2 * e + 1) * PB + 128, :] = z[:, 128:]
            swap_out(v2, g)
            return carry

        lax.fori_loop(0, 8, two, 0)

        def three(g, carry):
            for e in range(4):
                j = g * 8 + 2 * e
                y = dot(b1[...], jnp.concatenate([v2[j], v2[j + 1]], axis=1)).astype(BF16)
                vo[j] = y[:, :128]
                vo[j + 1] = y[:, 128:]
            return carry

        lax.fori_loop(0, 16, three, 0)

        stores = []
        for s in range(ND):
            dst = vs.at[ch, s] if s else q.at[ch, me]
            stores.append(pltpu.make_async_copy(
                vo.at[cols_of(s), rows_of(s), :], dst, vsem.at[s]))
            stores[-1].start()
        for store in stores:
            store.wait()
        for s in range(1, ND):
            back_copy(ch, s).start()
        return carry

    lax.fori_loop(0, ND, chunk, 0)

    for s in (2, 4, 6):
        d_out(s).wait_send()
    for s in (0, 2, 4, 6):
        d_relay(s).wait_send()

    def finish(ch, carry):
        for s in range(1, ND):
            out_copy(ch, s).wait_send()
            back_copy(ch, s).wait_send()
            back_arrival(ch, s).wait_recv()
        return carry

    lax.fori_loop(0, ND, finish, 0)


def exchange(x, w3, a1, a2, b2, b1, d):
    hbm = pl.BlockSpec(memory_space=pl.ANY)
    vmem = pl.BlockSpec(memory_space=pltpu.VMEM)
    dma = pltpu.SemaphoreType.DMA
    piece = (64, 32, 128)
    return pl.pallas_call(
        exchange_kernel,
        out_shape=[
            jax.ShapeDtypeStruct((4, 16) + piece, BF16),
            jax.ShapeDtypeStruct((ND, ND) + piece, BF16),
            jax.ShapeDtypeStruct((ND, ND) + piece, BF16),
            jax.ShapeDtypeStruct((ND, ND) + piece, BF16),
        ],
        in_specs=[hbm, vmem, vmem, vmem, vmem, vmem, hbm],
        out_specs=[hbm] * 4,
        scratch_shapes=[
            pltpu.VMEM((2, 32, JB, 16, 128), BF16),
            pltpu.VMEM((2, 16, JB, 32, 128), BF16),
            pltpu.VMEM((32 * PA, 128), F32),
            pltpu.VMEM((128, 128, 128), BF16),
            pltpu.VMEM((128, 128, 128), BF16),
            pltpu.VMEM((128, 128, 128), BF16),
            pltpu.VMEM((128, 128, 128), BF16),
            pltpu.VMEM((16 * PB, 128), F32),
            pltpu.VMEM((128, 128, 128), F32),
            dma((2,)), dma((2,)), dma((ND,)), dma((ND,)), dma(()),
            dma((ND,)), dma((ND,)),
            dma((ND, ND)), dma((ND, ND)), dma((ND, ND)), dma((ND, ND)),
        ],
        compiler_params=pltpu.CompilerParams(
            collective_id=0, has_side_effects=True, vmem_limit_bytes=56 * 1024 * 1024),
        name='exchange',
    )(x, w3, a1, a2, b2, b1, d)[3]


PC = JC * 32 + 8


def last_kernel(q, b3t, z, t):
    n = JC * 32
    y = dot(q[...].reshape(64 * n, 128), b3t[...])
    for r in range(64):
        t[r * PC:r * PC + n, :] = y[r * n:(r + 1) * n]

    for j in range(JC):
        for i in range(32):
            z[i, j] = t[pl.ds(j * 32 + i, 64, stride=PC), :]


def last(q, b3t):
    return pl.pallas_call(
        last_kernel,
        grid=(64 // JC,),
        out_shape=jax.ShapeDtypeStruct((32, 64, 64, 128), F32),
        in_specs=[
            pl.BlockSpec((64, JC, 32, 128), lambda j: (0, j, 0, 0)),
            pl.BlockSpec((128, 128), lambda j: (0, 0)),
        ],
        out_specs=pl.BlockSpec((32, JC, 64, 128), lambda j: (0, j, 0, 0)),
        scratch_shapes=[pltpu.VMEM((64 * PC, 128), F32)],
        compiler_params=pltpu.CompilerParams(vmem_limit_bytes=40 * 1024 * 1024),
        name='last',
    )(q, b3t)


def solution(mesh):
    vol_spec = P('row', 'col', None, 'rhs')
    diag_spec = P('row', 'col', None)
    full_spec = P(None, None)

    def local_op(volume, a_one, b_one, a_two, b_two, a_three, b_three, spectrum):
        x = jnp.transpose(volume, (0, 1, 3, 2))
        a3t = a_three.T
        zero = jnp.zeros_like(a3t)
        w3 = jnp.concatenate([jnp.concatenate([a3t, zero], 1), jnp.concatenate([zero, a3t], 1)], 0)
        q = exchange(x, w3, a_one, a_two, b_two, b_one, spectrum)
        z = last(q.reshape(64, 64, 32, 128), b_three.T)
        return jnp.transpose(z, (0, 1, 3, 2))

    return jax.shard_map(
        local_op, mesh=mesh,
        in_specs=(vol_spec, full_spec, full_spec, full_spec, full_spec, full_spec, full_spec, diag_spec),
        out_specs=vol_spec, check_vma=False)
```

time: 3340 us -> 825 us (0.25)
  local copies, waits for them, and re-layouts: 1610 us -> 0.98 us
  Pallas kernels: 0 us -> 820 us
  blocking collectives: 775 us -> 0 us
  waiting for transfers between devices: 702 us -> 0 us
  matrix products: 180 us -> 0 us
  starting transfers between devices: 42.8 us -> 0 us
    pallas_call x0 -> x2, Pallas kernels: none -> 820 us  [the longest x1 774 us: exchange(): pl.pallas_call(exchange_kernel, out_shape=[jax.ShapeDtypeStruct((4, 16) +...]
    all_to_all x2 -> x0, blocking collectives: 775 us -> none  [the longest x1 394 us: local_op(): one_again = lax.all_to_all(v_two, 'col', 1, 0, tiled=True)]
    all_to_all x4 -> x0, waiting for transfers between devices: 702 us -> none  [the longest x1 351 us: local_op(): one_whole = lax.all_to_all(u_three, 'row', 2, 0, tiled=True)]
    all_to_all x9 -> x0, local copies, waits for them, and re-layouts: 681 us -> none  [the longest x2 282 us: local_op(): two_whole = lax.all_to_all(u_one, 'col', 0, 1, tiled=True)]
    unnamed x27 -> x4, local copies, waits for them, and re-layouts: 565 us -> 0.98 us
    convert_element_type x4 -> x0, local copies, waits for them, and re-layouts: 357 us -> none  [the longest x1 89.9 us: local_op(): mode_product(a_three, volume, 'ka,ijar->ijkr').astype(jnp.bfloat16)]
    dot_general x5 -> x0, matrix products: 180 us -> none  [mode_product(): return jnp.einsum(form, factor, tensor, preferred_element_type=jnp.float32)]
    all_to_all x4 -> x0, starting transfers between devices: 42.8 us -> none  [the longest x1 20.6 us: local_op(): one_whole = lax.all_to_all(u_three, 'row', 2, 0, tiled=True)]
  transfers between devices with their start and end apart: 4 -> 0, of which waited for: 2 -> 0; matrix products, arithmetic and copies ran while one was open for 16% -> 0% of each run, Pallas kernels for 0% -> 0%
where the time goes in v1:
time: 825 us; the launch traced here: 822 us
  Pallas kernels  820 us (99%)
    pallas_call x1, Pallas kernels, exchange(): pl.pallas_call(exchange_kernel, out_shape=[jax.ShapeDtypeStruct((4, 16) +...  774 us
    pallas_call x1, Pallas kernels, last(): pl.pallas_call(last_kernel, grid=(64 // JC,), out_shape=jax.ShapeDtypeStr...  46.3 us

profile of v1, /device:TPU:0, one launch (start us, length us, event | category | flops | bytes accessed | tf_op | source)
XLA Modules:
  0.0 822.1 jit_solution(18314792651575016145)
XLA Ops:
  0.0 0.0 copy-start
  0.0 0.9 copy.9
  0.9 0.7 fusion.2.w3
  1.6 774.1 %exchange.1 = (bf16[4,16,64,32,128]{4,3,2,1,0:T(8,128)(2,1)}, bf16[8,8,64,32,128]{4,3,2,1,0:T(8,128)(2,1)}, bf16[8,8,64,32,128]{4,3,2,1,0:T(8,128)(2,1)}, bf16[8,8,64,32,128]{4,3,2,1,0:T(8,128)(2,1)}) custom-call(bf16[32,64,64,128]{3,2,1,0:T(8,128)(2,1)} %bitcast.6, bf16[256,256]{1,0:T(8,128)(2,1)} %fusion.2.w3, bf16[128,128]{1,0:T(8,128)(2,1)} %a1.1, ...), custom_call_target="tpu_custom_call" | custom-call | tf_op jit(solution)/shard_map/exchange/pallas_call | solution.py:236
  775.6 0.0 copy-done
  775.6 0.1 copy.10
  775.8 46.3 %last.1 = f32[32,64,64,128]{3,2,1,0:T(8,128)} custom-call(bf16[64,64,32,128]{3,2,1,0:T(8,128)(2,1)} %bitcast.7, bf16[128,128]{1,0:T(8,128)(2,1)S(1)} %bitcast.5), custom_call_target="tpu_custom_call" | custom-call | tf_op jit(solution)/shard_map/last/pallas_call | solution.py:281
Async XLA Ops:
  0.0 775.6 %copy-start = (bf16[128,128]{1,0:T(8,128)(2,1)S(1)}, bf16[128,128]{1,0:T(8,128)(2,1)}, u32[]{:S(2)}) copy-start(bf16[128,128]{1,0:T(8,128)(2,1)} %param.14) | copy-start | bytes 98308
